TPU v7x, 32 devices: a whole 2x2x4 slice. The times are simulated.
32 devices in a mesh: gx: 8 (over y, x, core), gy: 4 (over z).
Axes of the slice: x: 2, y: 2, z: 4, core: 2. Of those that a mesh axis runs over, the one named last changes fastest.
Arguments:
- adjoint: float32 [9, 32, 128, 512], P(None, 'gx', 'gy'), may hold values from -6 to 6
- buoyancy: float32 [32, 128, 512], P('gx', 'gy'), may hold values from 0.5 to 2
- lame_lambda: float32 [32, 128, 512], P('gx', 'gy'), may hold values from 0.5 to 2
- shear_mu: float32 [32, 128, 512], P('gx', 'gy'), may hold values from 0.3 to 1.2
- packed: int32 [8, 8, 4, 12, 2048], P('gx', None, 'gy'), may hold values from -2147483648 to 2147483646
- scales: float32 [8, 8, 4, 12], P('gx', None, 'gy'), may hold values from 0.005 to 0.05
- perm: int32 [8, 8], P('gx'), may hold values from 0 to 7, each once within a row
Outputs:
- adjoint_out: float32 [9, 32, 128, 512], P(None, 'gx', 'gy')
- gradients: float32 [2, 32, 128, 512], P(None, 'gx', 'gy')
Inputs may be any that keep to these rules, and one draw needn't show every extreme that they name: Each row of perm names every number 0 to 7 once. The words of packed are stored inputs and may cross devices as they are, four signed bytes to a word; only values that a program computes travel in float32.
All inputs are finite; a program needn't handle non-finite values.
Results may differ from a plain program's by a relative error of at most 0.0003.
Values sent between devices are 32-bit elements; how exact they have to be, the bound alone decides.
A program may use at most 128 MiB of HBM per device.

v0:
```python
import functools

import jax
import jax.numpy as jnp
from jax import lax
from jax.experimental import pallas as pl
from jax.experimental.pallas import tpu as pltpu
from jax.sharding import PartitionSpec as P

MESH = pl.DeviceIdType.MESH
STEPS = 2
COURANT = 0.15
ROWS = 8
PIECES = 2

VX, VY, VZ, SXX, SYY, SZZ, SXY, SXZ, SYZ = range(9)

STRESS_X = ((0, (SXX,), -1), (1, (SXY, SXZ), 1))
STRESS_Y = ((0, (SYY,), -1), (1, (SXY, SYZ), 1))
SPEED_X = ((3, (VY, VZ), -1), (5, (VX,), 1))
SPEED_Y = ((3, (VX, VZ), -1), (5, (VY,), 1))


def partner(me, distance, count):
    if count & (count - 1):
        return lax.rem(me + distance, count)
    result, bit = me, 1
    while bit < count:
        if distance & bit:
            result = result + bit - 2 * bit * ((me // bit) % 2)
        bit *= 2
    return result


def kernel(n_x, n_y, adj, buoy, lam, shear, packed, scales, perm, out, grads,
           cur, coef, strain, halo_x, halo_y, send_y, factors, factor_s, inv,
           in_sem, xs_sem, xr_sem, ys_sem, yr_sem, ws_sem, wr_sem, fs_sem, fr_sem, loc_sem, *words):
    cx, cy, cz = buoy.shape
    comp = packed.shape[1]
    per_step = comp // STEPS
    lanes = packed.shape[3]
    segw = packed.shape[2] * lanes
    tiles = cy // ROWS
    pieces = xs_sem.shape[1]
    part = cy // pieces
    me_x, me_y = lax.axis_index("gx"), lax.axis_index("gy")

    loads = []
    for index in (SXX, SXY, SXZ, SYY, SYZ, SZZ, VX, VY, VZ):
        loads.append(pltpu.make_async_copy(adj.at[index], cur.at[index, pl.ds(1, cx)], in_sem.at[index]))
    for index, ref in enumerate((buoy, lam, shear)):
        loads.append(pltpu.make_async_copy(ref, coef.at[index], in_sem.at[9 + index]))
    own_words = [pltpu.make_async_copy(packed.at[me_x, pl.ds(step * per_step, per_step)], words[step].at[me_x],
                                       loc_sem.at[2 + step]) for step in range(STEPS)]
    own_factor = pltpu.make_async_copy(scales.at[0, me_x], factors.at[me_x], loc_sem.at[1])
    for copy in loads:
        copy.start()
    for copy in own_words:
        copy.start()
    own_factor.start()

    barrier = pltpu.get_barrier_semaphore()
    for distance in range(1, n_x):
        pl.semaphore_signal(barrier, inc=1, device_id={"gx": partner(me_x, distance, n_x)}, device_id_type=MESH)

    def edge(way, axis):
        me, count = (me_x, n_x) if axis == "gx" else (me_y, n_y)
        return (me > 0) if way < 0 else (me < count - 1)

    for way in (-1, 1):
        @pl.when(edge(way, "gy"))
        def _():
            pl.semaphore_signal(barrier, inc=1, device_id={"gy": me_y + way}, device_id_type=MESH)

    pl.semaphore_wait(barrier, n_x - 1 + jnp.minimum(me_y, 1) + jnp.minimum(n_y - 1 - me_y, 1))

    def copy_x(step, message, source, piece):
        start, fields, way = message
        slot = 6 * step + start
        return pltpu.make_async_remote_copy(
            src_ref=source(fields, way, piece),
            dst_ref=halo_x.at[pl.ds(slot, len(fields)), pl.ds(piece * part, part)],
            send_sem=xs_sem.at[slot, piece], recv_sem=xr_sem.at[slot, piece],
            device_id={"gx": me_x + way}, device_id_type=MESH)

    def copy_y(step, message):
        start, fields, way = message
        slot = 6 * step + start
        return pltpu.make_async_remote_copy(
            src_ref=send_y.at[pl.ds(slot, len(fields))], dst_ref=halo_y.at[pl.ds(slot, len(fields))],
            send_sem=ys_sem.at[slot], recv_sem=yr_sem.at[slot],
            device_id={"gy": me_y + way}, device_id_type=MESH)

    def layer(fields, way, piece):
        return cur.at[pl.ds(fields[0], len(fields)), 1 if way < 0 else cx, pl.ds(piece * part, part)]

    def first_layer(fields, way, piece):
        return adj.at[pl.ds(fields[0], len(fields)), 0 if way < 0 else cx - 1, pl.ds(piece * part, part)]

    def word_copy(distance, step):
        to = partner(me_x, distance, n_x)
        stored = pl.ds(step * per_step, per_step)
        return pltpu.make_async_remote_copy(
            src_ref=packed.at[to, stored], dst_ref=words[step].at[me_x], send_sem=ws_sem.at[distance, step],
            recv_sem=wr_sem.at[distance, step], device_id={"gx": to}, device_id_type=MESH)

    def factor_copy(distance):
        to = partner(me_x, distance, n_x)
        return pltpu.make_async_remote_copy(
            src_ref=scales.at[0, to], dst_ref=factors.at[me_x], send_sem=fs_sem.at[distance],
            recv_sem=fr_sem.at[distance], device_id={"gx": to}, device_id_type=MESH)

    def send_x(step, messages, source, piece):
        for message in messages:
            @pl.when(edge(message[2], "gx"))
            def _():
                copy_x(step, message, source, piece).start()

    def send_rows(step, messages):
        for message in messages:
            start, fields, way = message

            @pl.when(edge(way, "gy"))
            def _():
                row = 0 if way < 0 else cy - 1
                for offset, field in enumerate(fields):
                    for x in range(cx):
                        send_y[6 * step + start + offset, pl.ds(x, 1), :] = cur[field, 1 + x, pl.ds(row, 1), :]
                copy_y(step, message).start()

    def finish_sends(step, messages_x, messages_y):
        for message in messages_x:
            @pl.when(edge(message[2], "gx"))
            def _():
                for piece in range(pieces):
                    copy_x(step, message, layer, piece).wait_send()
        for message in messages_y:
            @pl.when(edge(message[2], "gy"))
            def _():
                copy_y(step, message).wait_send()

    def receive_y(step, messages):
        for message in messages:
            start, fields, way = message

            @pl.when(edge(-way, "gy"))
            def _():
                copy_y(step, message).wait_recv()

            @pl.when(jnp.logical_not(edge(-way, "gy")))
            def _():
                for offset in range(len(fields)):
                    halo_y[6 * step + start + offset] = jnp.zeros((cx, cz), jnp.float32)

    def receive_x(step, messages, piece):
        rows = pl.ds(piece * part, part)
        for message in messages:
            start, fields, way = message
            place = cx + 1 if way < 0 else 0

            @pl.when(edge(-way, "gx"))
            def _():
                copy_x(step, message, layer, piece).wait_recv()
                for offset, field in enumerate(fields):
                    cur[field, place, rows, :] = halo_x[6 * step + start + offset, rows, :]

            @pl.when(jnp.logical_not(edge(-way, "gx")))
            def _():
                for field in fields:
                    cur[field, place, rows, :] = jnp.zeros((part, cz), jnp.float32)

    far = max(3 * n_x // 4, 1)

    def send_group(which):
        step, late = which // 2, which % 2
        for distance in range(2, n_x) if n_x > 2 else ():
            if (distance >= far) == (late == 1):
                word_copy(distance, step).start()
        if late == 1:
            word_copy(1, step).start()
        if which == 0:
            for distance in range(1, n_x):
                factor_copy(distance).start()

    def receive_words(step):
        if step == 0:
            own_factor.wait()
            for distance in range(1, n_x):
                factor_copy(distance).wait()
            to_scalar = pltpu.make_async_copy(factors, factor_s, loc_sem.at[0])
            to_scalar.start()
            to_scalar.wait()
        own_words[step].wait()
        for distance in range(1, n_x):
            word_copy(distance, step).wait()

    sub = lax.broadcasted_iota(jnp.int32, (ROWS, cz), 0)
    lane = lax.broadcasted_iota(jnp.int32, (ROWS, cz), 1)
    first_row, last_row = sub == 0, sub == ROWS - 1
    first_lane, last_lane = lane == 0, lane == cz - 1

    def tile(field, x, t):
        return cur[field, x + 1, pl.ds(t * ROWS, ROWS), :]

    def z_before(value):
        return jnp.where(first_lane, 0.0, pltpu.roll(value, 1, 1))

    def z_after(value):
        return jnp.where(last_lane, 0.0, pltpu.roll(value, cz - 1, 1))

    def y_before(value, field, x, t, slot):
        row = halo_y[slot, pl.ds(x, 1), :] if t == 0 else cur[field, x + 1, pl.ds(t * ROWS - 1, 1), :]
        return jnp.where(first_row, jnp.broadcast_to(row, value.shape), pltpu.roll(value, 1, 0))

    def y_after(value, field, x, t, slot):
        row = halo_y[slot, pl.ds(x, 1), :] if t == tiles - 1 else cur[field, x + 1, pl.ds(t * ROWS + ROWS, 1), :]
        return jnp.where(last_row, jnp.broadcast_to(row, value.shape), pltpu.roll(value, ROWS - 1, 0))

    def velocity(step, which, x):
        slot = 6 * step
        for t in which:
            rows = pl.ds(t * ROWS, ROWS)
            scaled = COURANT * coef[0, x, rows, :]
            sxy, sxz, syz = tile(SXY, x, t), tile(SXZ, x, t), tile(SYZ, x, t)
            sxx, syy, szz = tile(SXX, x, t), tile(SYY, x, t), tile(SZZ, x, t)
            moved = (
                tile(VX, x, t) - scaled * (
                    (tile(SXX, x + 1, t) - sxx) + (sxy - y_before(sxy, SXY, x, t, slot + 1)) + (sxz - z_before(sxz))),
                tile(VY, x, t) - scaled * (
                    (sxy - tile(SXY, x - 1, t)) + (y_after(syy, SYY, x, t, slot) - syy) + (syz - z_before(syz))),
                tile(VZ, x, t) - scaled * (
                    (sxz - tile(SXZ, x - 1, t)) + (syz - y_before(syz, SYZ, x, t, slot + 2)) + (z_after(szz) - szz)))
            for field, value in enumerate(moved):
                cur[field, x + 1, rows, :] = value
                if step == STEPS - 1:
                    out[field, x, rows, :] = value

    def stress(step, which, x):
        slot = 6 * step + 3
        for t in which:
            rows = pl.ds(t * ROWS, ROWS)
            vx, vy, vz = tile(VX, x, t), tile(VY, x, t), tile(VZ, x, t)
            exx = vx - tile(VX, x - 1, t)
            eyy = vy - y_before(vy, VY, x, t, slot + 2)
            ezz = vz - z_before(vz)
            exy = (y_after(vx, VX, x, t, slot) - vx) + (tile(VY, x + 1, t) - vy)
            exz = (z_after(vx) - vx) + (tile(VZ, x + 1, t) - vz)
            eyz = (z_after(vy) - vy) + (y_after(vz, VZ, x, t, slot + 1) - vz)
            both = (exx, eyy, ezz, exy, exz, eyz)
            for index, value in enumerate(both):
                strain[6 * step + index, x, rows, :] = value
            pull = (COURANT * coef[1, x, rows, :]) * (exx + eyy + ezz)
            mu = COURANT * coef[2, x, rows, :]
            for index, value in enumerate(both):
                change = pull + (2.0 * mu) * value if index < 3 else mu * value
                moved = tile(SXX + index, x, t) - change
                if step == STEPS - 1:
                    out[SXX + index, x, rows, :] = moved
                else:
                    cur[SXX + index, x + 1, rows, :] = moved

    def over(first, last, body):
        def run(x, carry):
            body(x)
            return carry
        lax.fori_loop(first, last, run, 0)

    def ends(body):
        def run(index, carry):
            body(index * (cx - 1))
            return carry
        lax.fori_loop(0, 2, run, 0)

    width = lanes
    per_x = cy * cz // (4 * segw)

    def source(row, chunk):
        offset = row * cz + chunk * width
        within = offset % (4 * segw)
        return offset // (4 * segw), within % segw, within // segw

    sub_w = lax.broadcasted_iota(jnp.int32, (ROWS, width), 0)

    def gradient(step, x):
        made = {}
        for t in range(tiles):
            for chunk in range(cz // width):
                rows = pl.ds(t * ROWS, ROWS)
                columns = pl.ds(chunk * width, width)
                plan = [source(t * ROWS + r, chunk) for r in range(ROWS)]
                shift = jnp.full((ROWS, width), 8 * plan[0][2], jnp.int32)
                for r in range(1, ROWS):
                    if plan[r][2] != plan[r - 1][2]:
                        shift = jnp.where(sub_w >= r, 8 * plan[r][2], shift)
                key = tuple(p[:2] for p in plan)
                distinct = list(dict.fromkeys(key))
                masks = []
                for item in distinct[1:]:
                    mask = None
                    for r in range(ROWS):
                        if key[r] == item:
                            mask = (sub_w == r) if mask is None else mask | (sub_w == r)
                    masks.append(mask)
                holders = {b: inv[x * per_x + b] for b in dict.fromkeys(k[0] for k in key)}
                blocks = [k[0] for k in key]

                def stored(c):
                    if (key, c) not in made:
                        word = None
                        for position, (block, start) in enumerate(distinct):
                            piece = jnp.broadcast_to(
                                words[step][holders[block], c - per_step * step, pl.ds(start // lanes, 1), :], (ROWS, width))
                            word = piece if word is None else jnp.where(masks[position - 1], piece, word)
                        made[key, c] = word ^ jnp.int32(-2147483648)
                    byte = (lax.shift_right_logical(made[key, c], shift) & 255) - 128
                    factor = None
                    for r in range(ROWS):
                        if r == 0:
                            factor = factor_s[holders[blocks[0]], 0, c]
                        elif blocks[r] != blocks[r - 1]:
                            factor = jnp.where(sub_w >= r, factor_s[holders[blocks[r]], 0, c], factor)
                    return byte.astype(jnp.float32) * factor

                e = [strain[6 * step + index, x, rows, columns] for index in range(6)]
                f = [stored(6 * step + index) for index in range(6)]
                grad_lambda = (e[0] + e[1] + e[2]) * (f[0] + f[1] + f[2])
                grad_mu = 2.0 * (e[0] * f[0] + e[1] * f[1] + e[2] * f[2])
                grad_mu = grad_mu + e[3] * f[3] + e[4] * f[4] + e[5] * f[5]
                if step > 0:
                    grad_lambda = grads[0, x, rows, columns] + grad_lambda
                    grad_mu = grads[1, x, rows, columns] + grad_mu
                grads[0, x, rows, columns] = grad_lambda
                grads[1, x, rows, columns] = grad_mu

    def inside(piece):
        return range(piece * part // ROWS, (piece + 1) * part // ROWS)

    outer = (0, tiles - 1) if tiles > 1 else (0,)
    inner = range(1, tiles - 1)

    for step in range(STEPS):
        if step == 0:
            for piece in range(pieces):
                send_x(0, STRESS_X, first_layer, piece)
            for copy in loads:
                copy.wait()
            send_rows(0, STRESS_Y)
            send_group(0)
            def invert(block, carry):
                total = jnp.int32(0)
                for holder in range(n_x):
                    total = jnp.where(perm[0, holder] == block, holder, total)
                inv[block] = total
                return carry
            lax.fori_loop(0, n_x, invert, 0)
        if step > 0:
            finish_sends(step - 1, SPEED_X, SPEED_Y)
        receive_y(step, STRESS_Y)
        for piece in range(pieces):
            receive_x(step, STRESS_X, piece)
            ends(functools.partial(velocity, step, inside(piece)))
            send_x(step, SPEED_X, layer, piece)
        over(1, cx - 1, functools.partial(velocity, step, outer))
        send_rows(step, SPEED_Y)
        over(1, cx - 1, functools.partial(velocity, step, inner))
        send_group(1 + 2 * step)
        if step > 0:
            receive_words(step - 1)
            over(0, cx, functools.partial(gradient, step - 1))
        finish_sends(step, STRESS_X, STRESS_Y)
        receive_y(step, SPEED_Y)
        for piece in range(pieces):
            receive_x(step, SPEED_X, piece)
            ends(functools.partial(stress, step, inside(piece)))
            if step < STEPS - 1:
                send_x(step + 1, STRESS_X, layer, piece)
        over(1, cx - 1, functools.partial(stress, step, outer))
        if step < STEPS - 1:
            send_rows(step + 1, STRESS_Y)
        over(1, cx - 1, functools.partial(stress, step, inner))
        if step < STEPS - 1:
            send_group(2 + 2 * step)
    finish_sends(STEPS - 1, SPEED_X, SPEED_Y)
    receive_words(STEPS - 1)
    over(0, cx, functools.partial(gradient, STEPS - 1))


def on_device(n_x, n_y, adjoint, buoyancy, lame_lambda, shear_mu, packed, scales, perm):
    fields, cx, cy, cz = adjoint.shape
    comp, segw = packed.shape[3:]
    lanes = min(128, segw)
    packed = packed.reshape(n_x, comp, segw // lanes, lanes)
    halos = 6 * STEPS
    pieces = PIECES if cy % (PIECES * ROWS) == 0 else 1
    dma = pltpu.SemaphoreType.DMA
    return pl.pallas_call(
        functools.partial(kernel, n_x, n_y),
        out_shape=(pltpu.VMEM(adjoint.shape, jnp.float32), pltpu.VMEM((2, cx, cy, cz), jnp.float32)),
        in_specs=[pl.BlockSpec(memory_space=pltpu.HBM)] * 6 + [pl.BlockSpec(memory_space=pltpu.SMEM)],
        out_specs=(pl.BlockSpec(memory_space=pltpu.VMEM),) * 2,
        scratch_shapes=[
            pltpu.VMEM((fields, cx + 2, cy, cz), jnp.float32),
            pltpu.VMEM((3, cx, cy, cz), jnp.float32),
            pltpu.VMEM((comp, cx, cy, cz), jnp.float32),
            pltpu.VMEM((halos, cy, cz), jnp.float32),
            pltpu.VMEM((halos, cx, cz), jnp.float32),
            pltpu.VMEM((halos, cx, cz), jnp.float32),
            pltpu.VMEM((n_x, 1, comp), jnp.float32),
            pltpu.SMEM((n_x, 1, comp), jnp.float32),
            pltpu.SMEM((n_x,), jnp.int32),
            dma((12,)), dma((halos, pieces)), dma((halos, pieces)), dma((halos,)), dma((halos,)),
            dma((n_x, STEPS)), dma((n_x, STEPS)), dma((n_x,)), dma((n_x,)), dma((2 + STEPS,)),
        ] + [pltpu.VMEM((n_x, comp // STEPS, segw // lanes, lanes), jnp.int32)] * STEPS,
        compiler_params=pltpu.CompilerParams(collective_id=0, has_side_effects=True,
                                             vmem_limit_bytes=64000000),
    )(adjoint, buoyancy, lame_lambda, shear_mu, packed, scales, perm)


def solution(mesh):
    return jax.shard_map(
        functools.partial(on_device, mesh.shape["gx"], mesh.shape["gy"]),
        mesh=mesh,
        in_specs=(
            P(None, "gx", "gy", None),
            P("gx", "gy", None),
            P("gx", "gy", None),
            P("gx", "gy", None),
            P("gx", None, "gy", None, None),
            P("gx", None, "gy", None),
            P("gx", None),
        ),
        out_specs=(P(None, "gx", "gy", None), P(None, "gx", "gy", None)),
        check_vma=False,
    )
```

profile of v0, /device:TPU:1, one launch (start us, length us, event | category | flops | bytes accessed | tf_op | source)
XLA Modules:
  0.0 26.9 jit_solution(5183668970919429755)
XLA Ops:
  0.6 24.1 %shard_map.86 = (f32[9,4,32,512]{3,2,1,0:T(8,128)S(1)}, f32[2,4,32,512]{3,2,1,0:T(8,128)S(1)}) custom-call(f32[9,4,32,512]{3,2,1,0:T(8,128)} %adj.1, f32[4,32,512]{2,1,0:T(8,128)} %buoy.1, f32[4,32,512]{2,1,0:T(8,128)} %lam.1, f32[4,32,512]{2,1,0:T(8,128)} %shear.1, s32[8,12,16,128]{3,2,1,0:T(8,128)} %bitcast.1, f32[1,8,1,12]{3,2,1,0:T(1,128)} %scales.1, ...), custom_call_target="tpu_custom_call" | custom-call | tf_op jit(solution)/shard_map/pallas_call | solution.py:396
  24.7 1.4 %copy.11 = f32[9,4,32,512]{3,2,1,0:T(8,128)} copy(f32[9,4,32,512]{3,2,1,0:T(8,128)S(1)} %get-tuple-element.2) | data formatting | bytes 4718592
  26.1 0.8 %copy.12 = f32[2,4,32,512]{3,2,1,0:T(8,128)} copy(f32[2,4,32,512]{3,2,1,0:T(8,128)S(1)} %get-tuple-element.3) | data formatting | bytes 1048576
where the time goes:
time: 27.1 us; the launch traced here: 26.9 us
  Pallas kernels  24.1 us (89%)
  local copies, waits for them, and re-layouts  2.2 us (8%)
  between operations  0.64 us (2%)
    pallas_call x1, Pallas kernels, on_device(): pl.pallas_call(functools.partial(kernel, n_x, n_y), out_shape=(pltpu.VMEM...  24.1 us
    unnamed x2, local copies, waits for them, and re-layouts  2.2 us

commit v1 on v0

--- a/solution.py
+++ b/solution.py
@@ -12,6 +12,14 @@
 COURANT = 0.15
 ROWS = 8
 PIECES = 2
+TURN = 6
+GROUPS = (
+    ((6, 0), (2, 0), (3, 0), (4, 0), (5, 0)),
+    ((7, 0), (2, 1), (6, 1), (1, 0), (4, 1)),
+    ((3, 1), (5, 1), (1, 1)),
+    ((7, 1),),
+)
+RELAYS = ((), (0,), (), (1,))
 
 VX, VY, VZ, SXX, SYY, SZZ, SXY, SXZ, SYZ = range(9)
 
@@ -32,9 +40,9 @@
     return result
 
 
-def kernel(n_x, n_y, adj, buoy, lam, shear, packed, scales, perm, out, grads,
-           cur, coef, strain, halo_x, halo_y, send_y, factors, factor_s, inv,
-           in_sem, xs_sem, xr_sem, ys_sem, yr_sem, ws_sem, wr_sem, fs_sem, fr_sem, loc_sem, *words):
+def kernel(n_x, n_y, adj, buoy, lam, shear, packed, scales, perm_in, out, grads,
+           cur, coef, strain, halo_y, send_y, relay, factors, factor_s, perm, inv,
+           in_sem, rl_sem, rf_sem, xs_sem, xr_sem, ys_sem, yr_sem, ws_sem, wr_sem, fs_sem, fr_sem, loc_sem, *words):
     cx, cy, cz = buoy.shape
     comp = packed.shape[1]
     per_step = comp // STEPS
@@ -46,18 +54,27 @@
     me_x, me_y = lax.axis_index("gx"), lax.axis_index("gy")
 
     loads = []
-    for index in (SXX, SXY, SXZ, SYY, SYZ, SZZ, VX, VY, VZ):
-        loads.append(pltpu.make_async_copy(adj.at[index], cur.at[index, pl.ds(1, cx)], in_sem.at[index]))
+
+    def load(sem, source, target):
+        copy = pltpu.make_async_copy(source, target, in_sem.at[sem])
+        loads.append(copy)
+        return copy
+
+    edges = [load(12, adj.at[SXX, 0], cur.at[SXX, 1]),
+             load(13, adj.at[pl.ds(SXY, 2), cx - 1], cur.at[pl.ds(SXY, 2), cx])]
+    rows_in = [load(SYY, adj.at[SYY], cur.at[SYY, pl.ds(1, cx)]),
+               load(SYZ, adj.at[SYZ], cur.at[SYZ, pl.ds(1, cx)]),
+               load(SXY, adj.at[pl.ds(SXY, 2), pl.ds(0, cx - 1)], cur.at[pl.ds(SXY, 2), pl.ds(1, cx - 1)])]
+    load(SXX, adj.at[SXX, pl.ds(1, cx - 1)], cur.at[SXX, pl.ds(2, cx - 1)])
+    for index in (SZZ, VX, VY, VZ):
+        load(index, adj.at[index], cur.at[index, pl.ds(1, cx)])
     for index, ref in enumerate((buoy, lam, shear)):
-        loads.append(pltpu.make_async_copy(ref, coef.at[index], in_sem.at[9 + index]))
+        load(9 + index, ref, coef.at[index])
     own_words = [pltpu.make_async_copy(packed.at[me_x, pl.ds(step * per_step, per_step)], words[step].at[me_x],
                                        loc_sem.at[2 + step]) for step in range(STEPS)]
     own_factor = pltpu.make_async_copy(scales.at[0, me_x], factors.at[me_x], loc_sem.at[1])
-    for copy in loads:
+    for copy in loads[:len(edges)]:
         copy.start()
-    for copy in own_words:
-        copy.start()
-    own_factor.start()
 
     barrier = pltpu.get_barrier_semaphore()
     for distance in range(1, n_x):
@@ -72,14 +89,28 @@
         def _():
             pl.semaphore_signal(barrier, inc=1, device_id={"gy": me_y + way}, device_id_type=MESH)
 
+    for copy in loads[len(edges):]:
+        copy.start()
+    perm_copy = pltpu.make_async_copy(perm_in, perm, loc_sem.at[2 + STEPS])
+    perm_copy.start()
+    for copy in own_words:
+        copy.start()
+    own_factor.start()
+    for way, place in ((-1, 0), (1, cx + 1)):
+        @pl.when(jnp.logical_not(edge(way, "gx")))
+        def _():
+            for field in (VX, SXY, SXZ) if way < 0 else (VY, VZ, SXX):
+                cur[field, place] = jnp.zeros((cy, cz), jnp.float32)
+
     pl.semaphore_wait(barrier, n_x - 1 + jnp.minimum(me_y, 1) + jnp.minimum(n_y - 1 - me_y, 1))
 
-    def copy_x(step, message, source, piece):
+    def copy_x(step, message, piece):
         start, fields, way = message
         slot = 6 * step + start
+        rows = pl.ds(piece * part, part)
         return pltpu.make_async_remote_copy(
-            src_ref=source(fields, way, piece),
-            dst_ref=halo_x.at[pl.ds(slot, len(fields)), pl.ds(piece * part, part)],
+            src_ref=cur.at[pl.ds(fields[0], len(fields)), 1 if way < 0 else cx, rows],
+            dst_ref=cur.at[pl.ds(fields[0], len(fields)), cx + 1 if way < 0 else 0, rows],
             send_sem=xs_sem.at[slot, piece], recv_sem=xr_sem.at[slot, piece],
             device_id={"gx": me_x + way}, device_id_type=MESH)
 
@@ -91,12 +122,6 @@
             send_sem=ys_sem.at[slot], recv_sem=yr_sem.at[slot],
             device_id={"gy": me_y + way}, device_id_type=MESH)
 
-    def layer(fields, way, piece):
-        return cur.at[pl.ds(fields[0], len(fields)), 1 if way < 0 else cx, pl.ds(piece * part, part)]
-
-    def first_layer(fields, way, piece):
-        return adj.at[pl.ds(fields[0], len(fields)), 0 if way < 0 else cx - 1, pl.ds(piece * part, part)]
-
     def word_copy(distance, step):
         to = partner(me_x, distance, n_x)
         stored = pl.ds(step * per_step, per_step)
@@ -110,11 +135,11 @@
             src_ref=scales.at[0, to], dst_ref=factors.at[me_x], send_sem=fs_sem.at[distance],
             recv_sem=fr_sem.at[distance], device_id={"gx": to}, device_id_type=MESH)
 
-    def send_x(step, messages, source, piece):
+    def send_x(step, messages, piece):
         for message in messages:
             @pl.when(edge(message[2], "gx"))
             def _():
-                copy_x(step, message, source, piece).start()
+                copy_x(step, message, piece).start()
 
     def send_rows(step, messages):
         for message in messages:
@@ -133,7 +158,7 @@
             @pl.when(edge(message[2], "gx"))
             def _():
                 for piece in range(pieces):
-                    copy_x(step, message, layer, piece).wait_send()
+                    copy_x(step, message, piece).wait_send()
         for message in messages_y:
             @pl.when(edge(message[2], "gy"))
             def _():
@@ -153,31 +178,47 @@
                     halo_y[6 * step + start + offset] = jnp.zeros((cx, cz), jnp.float32)
 
     def receive_x(step, messages, piece):
-        rows = pl.ds(piece * part, part)
         for message in messages:
-            start, fields, way = message
-            place = cx + 1 if way < 0 else 0
-
-            @pl.when(edge(-way, "gx"))
-            def _():
-                copy_x(step, message, layer, piece).wait_recv()
-                for offset, field in enumerate(fields):
-                    cur[field, place, rows, :] = halo_x[6 * step + start + offset, rows, :]
-
-            @pl.when(jnp.logical_not(edge(-way, "gx")))
-            def _():
-                for field in fields:
-                    cur[field, place, rows, :] = jnp.zeros((part, cz), jnp.float32)
-
-    far = max(3 * n_x // 4, 1)
+            @pl.when(edge(-message[2], "gx"))
+            def _():
+                copy_x(step, message, piece).wait_recv()
+
+    relays = n_x > TURN and n_x & (n_x - 1) == 0
+    bent = (me_x // (TURN & -TURN)) % 2 != (me_x // (TURN - (TURN & -TURN))) % 2
+    low, high = TURN & -TURN, TURN - (TURN & -TURN)
+
+    def first_leg(step):
+        return pltpu.make_async_remote_copy(
+            src_ref=packed.at[partner(me_x, TURN, n_x), pl.ds(step * per_step, per_step)], dst_ref=relay.at[step],
+            send_sem=ws_sem.at[TURN, step], recv_sem=rl_sem.at[step],
+            device_id={"gx": partner(me_x, high, n_x)}, device_id_type=MESH)
+
+    def second_leg(step):
+        return pltpu.make_async_remote_copy(
+            src_ref=relay.at[step], dst_ref=words[step].at[partner(me_x, high, n_x)],
+            send_sem=rf_sem.at[step], recv_sem=wr_sem.at[TURN, step],
+            device_id={"gx": partner(me_x, low, n_x)}, device_id_type=MESH)
 
     def send_group(which):
-        step, late = which // 2, which % 2
-        for distance in range(2, n_x) if n_x > 2 else ():
-            if (distance >= far) == (late == 1):
-                word_copy(distance, step).start()
-        if late == 1:
-            word_copy(1, step).start()
+        for kind, step in GROUPS[which]:
+            for distance in range(1, n_x):
+                if max(distance * 8 // n_x, 1) == kind:
+                    if relays and distance == TURN:
+                        @pl.when(bent)
+                        def _():
+                            first_leg(step).start()
+
+                        @pl.when(jnp.logical_not(bent))
+                        def _():
+                            word_copy(distance, step).start()
+                    else:
+                        word_copy(distance, step).start()
+        if relays:
+            for step in RELAYS[which]:
+                @pl.when(jnp.logical_not(bent))
+                def _():
+                    first_leg(step).wait_recv()
+                    second_leg(step).start()
         if which == 0:
             for distance in range(1, n_x):
                 factor_copy(distance).start()
@@ -193,6 +234,10 @@
         own_words[step].wait()
         for distance in range(1, n_x):
             word_copy(distance, step).wait()
+        if relays:
+            @pl.when(jnp.logical_not(bent))
+            def _():
+                second_leg(step).wait_send()
 
     sub = lax.broadcasted_iota(jnp.int32, (ROWS, cz), 0)
     lane = lax.broadcasted_iota(jnp.int32, (ROWS, cz), 1)
@@ -337,52 +382,68 @@
 
     outer = (0, tiles - 1) if tiles > 1 else (0,)
     inner = range(1, tiles - 1)
+    outside = [piece for piece in range(pieces) if set(inside(piece)) & set(outer)]
+    within = [piece for piece in range(pieces) if piece not in outside]
+
+    def phase(step, body, taken, taken_y, given_step, given, given_y):
+        over(1, cx - 1, functools.partial(body, step, inner))
+        for piece in within + outside:
+            if piece == outside[0]:
+                receive_y(step, taken_y)
+            receive_x(step, taken, piece)
+            ends(functools.partial(body, step, inside(piece)))
+            if given:
+                send_x(given_step, given, piece)
+        over(1, cx - 1, functools.partial(body, step, outer))
+        if given:
+            send_rows(given_step, given_y)
+
+    for copy in edges:
+        copy.wait()
+    for piece in within + outside:
+        send_x(0, STRESS_X, piece)
+    for copy in rows_in:
+        copy.wait()
+    send_rows(0, STRESS_Y)
+    send_group(0)
+    perm_copy.wait()
+
+    def invert(block, carry):
+        total = jnp.int32(0)
+        for holder in range(n_x):
+            total = jnp.where(perm[0, holder] == block, holder, total)
+        inv[block] = total
+        return carry
+    lax.fori_loop(0, n_x, invert, 0)
+    for copy in loads[len(edges) + len(rows_in):]:
+        copy.wait()
 
     for step in range(STEPS):
-        if step == 0:
-            for piece in range(pieces):
-                send_x(0, STRESS_X, first_layer, piece)
-            for copy in loads:
-                copy.wait()
-            send_rows(0, STRESS_Y)
-            send_group(0)
-            def invert(block, carry):
-                total = jnp.int32(0)
-                for holder in range(n_x):
-                    total = jnp.where(perm[0, holder] == block, holder, total)
-                inv[block] = total
-                return carry
-            lax.fori_loop(0, n_x, invert, 0)
+        last = step == STEPS - 1
         if step > 0:
             finish_sends(step - 1, SPEED_X, SPEED_Y)
-        receive_y(step, STRESS_Y)
-        for piece in range(pieces):
-            receive_x(step, STRESS_X, piece)
-            ends(functools.partial(velocity, step, inside(piece)))
-            send_x(step, SPEED_X, layer, piece)
-        over(1, cx - 1, functools.partial(velocity, step, outer))
-        send_rows(step, SPEED_Y)
-        over(1, cx - 1, functools.partial(velocity, step, inner))
+        phase(step, velocity, STRESS_X, STRESS_Y, step, SPEED_X, SPEED_Y)
         send_group(1 + 2 * step)
         if step > 0:
             receive_words(step - 1)
             over(0, cx, functools.partial(gradient, step - 1))
         finish_sends(step, STRESS_X, STRESS_Y)
-        receive_y(step, SPEED_Y)
-        for piece in range(pieces):
-            receive_x(step, SPEED_X, piece)
-            ends(functools.partial(stress, step, inside(piece)))
-            if step < STEPS - 1:
-                send_x(step + 1, STRESS_X, layer, piece)
-        over(1, cx - 1, functools.partial(stress, step, outer))
-        if step < STEPS - 1:
-            send_rows(step + 1, STRESS_Y)
-        over(1, cx - 1, functools.partial(stress, step, inner))
-        if step < STEPS - 1:
+        phase(step, stress, SPEED_X, SPEED_Y, step + 1, () if last else STRESS_X, STRESS_Y)
+        if not last:
             send_group(2 + 2 * step)
     finish_sends(STEPS - 1, SPEED_X, SPEED_Y)
     receive_words(STEPS - 1)
     over(0, cx, functools.partial(gradient, STEPS - 1))
+
+
+def flush(out_in, grads_in, out, grads, sem):
+    copies = [pltpu.make_async_copy(out_in.at[index], out.at[index], sem.at[index]) for index in range(out.shape[0])]
+    copies += [pltpu.make_async_copy(grads_in.at[index], grads.at[index], sem.at[out.shape[0] + index])
+               for index in range(grads.shape[0])]
+    for copy in copies:
+        copy.start()
+    for copy in copies:
+        copy.wait()
 
 
 def on_device(n_x, n_y, adjoint, buoyancy, lame_lambda, shear_mu, packed, scales, perm):
@@ -393,27 +454,36 @@
     halos = 6 * STEPS
     pieces = PIECES if cy % (PIECES * ROWS) == 0 else 1
     dma = pltpu.SemaphoreType.DMA
-    return pl.pallas_call(
+    held = pl.pallas_call(
         functools.partial(kernel, n_x, n_y),
         out_shape=(pltpu.VMEM(adjoint.shape, jnp.float32), pltpu.VMEM((2, cx, cy, cz), jnp.float32)),
-        in_specs=[pl.BlockSpec(memory_space=pltpu.HBM)] * 6 + [pl.BlockSpec(memory_space=pltpu.SMEM)],
+        in_specs=[pl.BlockSpec(memory_space=pltpu.HBM)] * 7,
         out_specs=(pl.BlockSpec(memory_space=pltpu.VMEM),) * 2,
         scratch_shapes=[
             pltpu.VMEM((fields, cx + 2, cy, cz), jnp.float32),
             pltpu.VMEM((3, cx, cy, cz), jnp.float32),
             pltpu.VMEM((comp, cx, cy, cz), jnp.float32),
-            pltpu.VMEM((halos, cy, cz), jnp.float32),
             pltpu.VMEM((halos, cx, cz), jnp.float32),
             pltpu.VMEM((halos, cx, cz), jnp.float32),
+            pltpu.VMEM((STEPS, comp // STEPS, segw // lanes, lanes), jnp.int32),
             pltpu.VMEM((n_x, 1, comp), jnp.float32),
             pltpu.SMEM((n_x, 1, comp), jnp.float32),
+            pltpu.SMEM(perm.shape, jnp.int32),
             pltpu.SMEM((n_x,), jnp.int32),
-            dma((12,)), dma((halos, pieces)), dma((halos, pieces)), dma((halos,)), dma((halos,)),
-            dma((n_x, STEPS)), dma((n_x, STEPS)), dma((n_x,)), dma((n_x,)), dma((2 + STEPS,)),
+            dma((14,)), dma((STEPS,)), dma((STEPS,)), dma((halos, pieces)), dma((halos, pieces)), dma((halos,)), dma((halos,)),
+            dma((n_x, STEPS)), dma((n_x, STEPS)), dma((n_x,)), dma((n_x,)), dma((3 + STEPS,)),
         ] + [pltpu.VMEM((n_x, comp // STEPS, segw // lanes, lanes), jnp.int32)] * STEPS,
         compiler_params=pltpu.CompilerParams(collective_id=0, has_side_effects=True,
                                              vmem_limit_bytes=64000000),
     )(adjoint, buoyancy, lame_lambda, shear_mu, packed, scales, perm)
+    return pl.pallas_call(
+        flush,
+        out_shape=tuple(jax.ShapeDtypeStruct(array.shape, jnp.float32) for array in held),
+        in_specs=[pl.BlockSpec(memory_space=pltpu.VMEM)] * 2,
+        out_specs=(pl.BlockSpec(memory_space=pltpu.HBM),) * 2,
+        scratch_shapes=[dma((fields + 2,))],
+        compiler_params=pltpu.CompilerParams(vmem_limit_bytes=1000000),
+    )(*held)
 
 
 def solution(mesh):

time: 27.1 us -> 25.1 us (0.926)
  local copies, waits for them, and re-layouts: 2.2 us -> 0 us
    unnamed x2 -> x0, local copies, waits for them, and re-layouts: 2.2 us -> none
    pallas_call x0 -> x1, Pallas kernels: none -> 1.66 us  [on_device(): pl.pallas_call(flush, out_shape=tuple((jax.ShapeDtypeStruct(array.shape,...]
    pallas_call x1, Pallas kernels: 24.1 us -> 22.6 us  [on_device(): pl.pallas_call(functools.partial(kernel, n_x, n_y), out_shape=(pltpu.VMEM...]
where the time goes in v1:
time: 25.1 us; the launch traced here: 24.9 us
  Pallas kernels  24.3 us (97%)
  between operations  0.64 us (3%)
    pallas_call x1, Pallas kernels, on_device(): pl.pallas_call(functools.partial(kernel, n_x, n_y), out_shape=(pltpu.VMEM...  22.6 us
    pallas_call x1, Pallas kernels, on_device(): pl.pallas_call(flush, out_shape=tuple((jax.ShapeDtypeStruct(array.shape,...  1.66 us

profile of v1, /device:TPU:1, one launch (start us, length us, event | category | flops | bytes accessed | tf_op | source)
XLA Modules:
  0.0 24.9 jit_solution(2762935169288580706)
XLA Ops:
  0.6 22.6 %shard_map.86 = (f32[9,4,32,512]{3,2,1,0:T(8,128)S(1)}, f32[2,4,32,512]{3,2,1,0:T(8,128)S(1)}) custom-call(f32[9,4,32,512]{3,2,1,0:T(8,128)} %adj.1, f32[4,32,512]{2,1,0:T(8,128)} %buoy.1, f32[4,32,512]{2,1,0:T(8,128)} %lam.1, f32[4,32,512]{2,1,0:T(8,128)} %shear.1, s32[8,12,16,128]{3,2,1,0:T(8,128)} %bitcast.1, f32[1,8,1,12]{3,2,1,0:T(1,128)} %scales.1, ...), custom_call_target="tpu_custom_call" | custom-call | tf_op jit(solution)/shard_map/pallas_call | solution.py:457
  23.2 1.7 %shard_map.87 = (f32[9,4,32,512]{3,2,1,0:T(8,128)}, f32[2,4,32,512]{3,2,1,0:T(8,128)}) custom-call(f32[9,4,32,512]{3,2,1,0:T(8,128)S(1)} %get-tuple-element.4.out_in, f32[2,4,32,512]{3,2,1,0:T(8,128)S(1)} %get-tuple-element.5.grads_in), custom_call_target="tpu_custom_call" | custom-call | tf_op jit(solution)/shard_map/pallas_call | solution.py:479

commit v2 on v1

--- a/solution.py
+++ b/solution.py
@@ -12,14 +12,10 @@
 COURANT = 0.15
 ROWS = 8
 PIECES = 2
+VMEM_LIMIT = 60500000
 TURN = 6
-GROUPS = (
-    ((6, 0), (2, 0), (3, 0), (4, 0), (5, 0)),
-    ((7, 0), (2, 1), (6, 1), (1, 0), (4, 1)),
-    ((3, 1), (5, 1), (1, 1)),
-    ((7, 1),),
-)
-RELAYS = ((), (0,), (), (1,))
+BENT = (((6, 0), (4, 0), (5, 0), (2, 0), (3, 0)), ((6, 1), (7, 0), (2, 1), (1, 0)), ((4, 1), (5, 1), (3, 1), (7, 1), (1, 1)), ())
+STRAIGHT = (((4, 0), (5, 0), (6, 0), (2, 0), (3, 0)), ((4, 1), (7, 0), (2, 1), (1, 0), (0, 0)), ((5, 1), (3, 1), (6, 1), (7, 1), (1, 1)), ((0, 1),))
 
 VX, VY, VZ, SXX, SYY, SZZ, SXY, SXZ, SYZ = range(9)
 
@@ -40,8 +36,64 @@
     return result
 
 
-def kernel(n_x, n_y, adj, buoy, lam, shear, packed, scales, perm_in, out, grads,
-           cur, coef, strain, halo_y, send_y, relay, factors, factor_s, perm, inv,
+def stencil(cur, coef, halo_y):
+    cx, cy, cz = coef.shape[1:]
+    tiles = cy // ROWS
+    sub = lax.broadcasted_iota(jnp.int32, (ROWS, cz), 0)
+    lane = lax.broadcasted_iota(jnp.int32, (ROWS, cz), 1)
+    first_row, last_row = sub == 0, sub == ROWS - 1
+    first_lane, last_lane = lane == 0, lane == cz - 1
+
+    def tile(field, x, t):
+        return cur[field, x + 1, pl.ds(t * ROWS, ROWS), :]
+
+    def z_before(value):
+        return jnp.where(first_lane, 0.0, pltpu.roll(value, 1, 1))
+
+    def z_after(value):
+        return jnp.where(last_lane, 0.0, pltpu.roll(value, cz - 1, 1))
+
+    def y_before(value, field, x, t, slot):
+        row = halo_y[slot, pl.ds(x, 1), :] if t == 0 else cur[field, x + 1, pl.ds(t * ROWS - 1, 1), :]
+        return jnp.where(first_row, jnp.broadcast_to(row, value.shape), pltpu.roll(value, 1, 0))
+
+    def y_after(value, field, x, t, slot):
+        row = halo_y[slot, pl.ds(x, 1), :] if t == tiles - 1 else cur[field, x + 1, pl.ds(t * ROWS + ROWS, 1), :]
+        return jnp.where(last_row, jnp.broadcast_to(row, value.shape), pltpu.roll(value, ROWS - 1, 0))
+
+    def strains(step, x, t):
+        slot = 6 * step + 3
+        vx, vy, vz = tile(VX, x, t), tile(VY, x, t), tile(VZ, x, t)
+        exx = vx - tile(VX, x - 1, t)
+        eyy = vy - y_before(vy, VY, x, t, slot + 2)
+        ezz = vz - z_before(vz)
+        exy = (y_after(vx, VX, x, t, slot) - vx) + (tile(VY, x + 1, t) - vy)
+        exz = (z_after(vx) - vx) + (tile(VZ, x + 1, t) - vz)
+        eyz = (z_after(vy) - vy) + (y_after(vz, VZ, x, t, slot + 1) - vz)
+        return exx, eyy, ezz, exy, exz, eyz
+
+    def stresses(both, x, t):
+        rows = pl.ds(t * ROWS, ROWS)
+        exx, eyy, ezz = both[:3]
+        pull = (COURANT * coef[1, x, rows, :]) * (exx + eyy + ezz)
+        mu = COURANT * coef[2, x, rows, :]
+        moved = []
+        for index, value in enumerate(both):
+            change = pull + (2.0 * mu) * value if index < 3 else mu * value
+            moved.append(tile(SXX + index, x, t) - change)
+        return moved
+
+    return tile, z_before, z_after, y_before, y_after, strains, stresses
+
+
+def products(e, f):
+    grad_lambda = (e[0] + e[1] + e[2]) * (f[0] + f[1] + f[2])
+    grad_mu = 2.0 * (e[0] * f[0] + e[1] * f[1] + e[2] * f[2])
+    return grad_lambda, grad_mu + e[3] * f[3] + e[4] * f[4] + e[5] * f[5]
+
+
+def kernel(n_x, n_y, adj, buoy, lam, shear, packed, scales, perm_in, cur, coef, halo_y, fwd, grads,
+           strain, send_y, relay, factors, factor_s, perm, inv,
            in_sem, rl_sem, rf_sem, xs_sem, xr_sem, ys_sem, yr_sem, ws_sem, wr_sem, fs_sem, fr_sem, loc_sem, *words):
     cx, cy, cz = buoy.shape
     comp = packed.shape[1]
@@ -199,26 +251,29 @@
             send_sem=rf_sem.at[step], recv_sem=wr_sem.at[TURN, step],
             device_id={"gx": partner(me_x, low, n_x)}, device_id_type=MESH)
 
-    def send_group(which):
-        for kind, step in GROUPS[which]:
+    def send_words(table, turned):
+        for kind, step in table:
+            if kind == 0 and relays:
+                first_leg(step).wait_recv()
+                second_leg(step).start()
             for distance in range(1, n_x):
                 if max(distance * 8 // n_x, 1) == kind:
-                    if relays and distance == TURN:
-                        @pl.when(bent)
-                        def _():
-                            first_leg(step).start()
-
-                        @pl.when(jnp.logical_not(bent))
-                        def _():
-                            word_copy(distance, step).start()
+                    if turned and distance == TURN:
+                        first_leg(step).start()
                     else:
                         word_copy(distance, step).start()
+
+    def send_group(which):
         if relays:
-            for step in RELAYS[which]:
-                @pl.when(jnp.logical_not(bent))
-                def _():
-                    first_leg(step).wait_recv()
-                    second_leg(step).start()
+            @pl.when(bent)
+            def _():
+                send_words(BENT[which], True)
+
+            @pl.when(jnp.logical_not(bent))
+            def _():
+                send_words(STRAIGHT[which], False)
+        else:
+            send_words(STRAIGHT[which], False)
         if which == 0:
             for distance in range(1, n_x):
                 factor_copy(distance).start()
@@ -239,27 +294,7 @@
             def _():
                 second_leg(step).wait_send()
 
-    sub = lax.broadcasted_iota(jnp.int32, (ROWS, cz), 0)
-    lane = lax.broadcasted_iota(jnp.int32, (ROWS, cz), 1)
-    first_row, last_row = sub == 0, sub == ROWS - 1
-    first_lane, last_lane = lane == 0, lane == cz - 1
-
-    def tile(field, x, t):
-        return cur[field, x + 1, pl.ds(t * ROWS, ROWS), :]
-
-    def z_before(value):
-        return jnp.where(first_lane, 0.0, pltpu.roll(value, 1, 1))
-
-    def z_after(value):
-        return jnp.where(last_lane, 0.0, pltpu.roll(value, cz - 1, 1))
-
-    def y_before(value, field, x, t, slot):
-        row = halo_y[slot, pl.ds(x, 1), :] if t == 0 else cur[field, x + 1, pl.ds(t * ROWS - 1, 1), :]
-        return jnp.where(first_row, jnp.broadcast_to(row, value.shape), pltpu.roll(value, 1, 0))
-
-    def y_after(value, field, x, t, slot):
-        row = halo_y[slot, pl.ds(x, 1), :] if t == tiles - 1 else cur[field, x + 1, pl.ds(t * ROWS + ROWS, 1), :]
-        return jnp.where(last_row, jnp.broadcast_to(row, value.shape), pltpu.roll(value, ROWS - 1, 0))
+    tile, z_before, z_after, y_before, y_after, strains, stresses = stencil(cur, coef, halo_y)
 
     def velocity(step, which, x):
         slot = 6 * step
@@ -277,32 +312,15 @@
                     (sxz - tile(SXZ, x - 1, t)) + (syz - y_before(syz, SYZ, x, t, slot + 2)) + (z_after(szz) - szz)))
             for field, value in enumerate(moved):
                 cur[field, x + 1, rows, :] = value
-                if step == STEPS - 1:
-                    out[field, x, rows, :] = value
 
     def stress(step, which, x):
-        slot = 6 * step + 3
         for t in which:
             rows = pl.ds(t * ROWS, ROWS)
-            vx, vy, vz = tile(VX, x, t), tile(VY, x, t), tile(VZ, x, t)
-            exx = vx - tile(VX, x - 1, t)
-            eyy = vy - y_before(vy, VY, x, t, slot + 2)
-            ezz = vz - z_before(vz)
-            exy = (y_after(vx, VX, x, t, slot) - vx) + (tile(VY, x + 1, t) - vy)
-            exz = (z_after(vx) - vx) + (tile(VZ, x + 1, t) - vz)
-            eyz = (z_after(vy) - vy) + (y_after(vz, VZ, x, t, slot + 1) - vz)
-            both = (exx, eyy, ezz, exy, exz, eyz)
+            both = strains(step, x, t)
             for index, value in enumerate(both):
                 strain[6 * step + index, x, rows, :] = value
-            pull = (COURANT * coef[1, x, rows, :]) * (exx + eyy + ezz)
-            mu = COURANT * coef[2, x, rows, :]
-            for index, value in enumerate(both):
-                change = pull + (2.0 * mu) * value if index < 3 else mu * value
-                moved = tile(SXX + index, x, t) - change
-                if step == STEPS - 1:
-                    out[SXX + index, x, rows, :] = moved
-                else:
-                    cur[SXX + index, x + 1, rows, :] = moved
+            for index, value in enumerate(stresses(both, x, t)):
+                cur[SXX + index, x + 1, rows, :] = value
 
     def over(first, last, body):
         def run(x, carry):
@@ -326,7 +344,7 @@
 
     sub_w = lax.broadcasted_iota(jnp.int32, (ROWS, width), 0)
 
-    def gradient(step, x):
+    def gradient(step, keep, x):
         made = {}
         for t in range(tiles):
             for chunk in range(cz // width):
@@ -366,16 +384,18 @@
                             factor = jnp.where(sub_w >= r, factor_s[holders[blocks[r]], 0, c], factor)
                     return byte.astype(jnp.float32) * factor
 
-                e = [strain[6 * step + index, x, rows, columns] for index in range(6)]
                 f = [stored(6 * step + index) for index in range(6)]
-                grad_lambda = (e[0] + e[1] + e[2]) * (f[0] + f[1] + f[2])
-                grad_mu = 2.0 * (e[0] * f[0] + e[1] * f[1] + e[2] * f[2])
-                grad_mu = grad_mu + e[3] * f[3] + e[4] * f[4] + e[5] * f[5]
-                if step > 0:
-                    grad_lambda = grads[0, x, rows, columns] + grad_lambda
-                    grad_mu = grads[1, x, rows, columns] + grad_mu
-                grads[0, x, rows, columns] = grad_lambda
-                grads[1, x, rows, columns] = grad_mu
+                if keep:
+                    for index, value in enumerate(f):
+                        fwd[index, x, rows, columns] = value
+                else:
+                    e = [strain[6 * step + index, x, rows, columns] for index in range(6)]
+                    grad_lambda, grad_mu = products(e, f)
+                    if step > 0:
+                        grad_lambda = grads[0, x, rows, columns] + grad_lambda
+                        grad_mu = grads[1, x, rows, columns] + grad_mu
+                    grads[0, x, rows, columns] = grad_lambda
+                    grads[1, x, rows, columns] = grad_mu
 
     def inside(piece):
         return range(piece * part // ROWS, (piece + 1) * part // ROWS)
@@ -385,27 +405,25 @@
     outside = [piece for piece in range(pieces) if set(inside(piece)) & set(outer)]
     within = [piece for piece in range(pieces) if piece not in outside]
 
-    def phase(step, body, taken, taken_y, given_step, given, given_y):
+    def phase(step, body, taken, taken_y, given_step, given, given_y, group):
         over(1, cx - 1, functools.partial(body, step, inner))
+        receive_y(step, taken_y)
+        over(1, cx - 1, functools.partial(body, step, outer))
         for piece in within + outside:
-            if piece == outside[0]:
-                receive_y(step, taken_y)
             receive_x(step, taken, piece)
             ends(functools.partial(body, step, inside(piece)))
-            if given:
-                send_x(given_step, given, piece)
-        over(1, cx - 1, functools.partial(body, step, outer))
-        if given:
-            send_rows(given_step, given_y)
+            send_x(given_step, given, piece)
+        send_rows(given_step, given_y)
+        send_group(group)
 
     for copy in edges:
         copy.wait()
     for piece in within + outside:
         send_x(0, STRESS_X, piece)
+    send_group(0)
     for copy in rows_in:
         copy.wait()
     send_rows(0, STRESS_Y)
-    send_group(0)
     perm_copy.wait()
 
     def invert(block, carry):
@@ -418,30 +436,53 @@
     for copy in loads[len(edges) + len(rows_in):]:
         copy.wait()
 
+    final = STEPS - 1
     for step in range(STEPS):
-        last = step == STEPS - 1
         if step > 0:
             finish_sends(step - 1, SPEED_X, SPEED_Y)
-        phase(step, velocity, STRESS_X, STRESS_Y, step, SPEED_X, SPEED_Y)
-        send_group(1 + 2 * step)
+        phase(step, velocity, STRESS_X, STRESS_Y, step, SPEED_X, SPEED_Y, 1 + 2 * step)
         if step > 0:
             receive_words(step - 1)
-            over(0, cx, functools.partial(gradient, step - 1))
+            over(0, cx, functools.partial(gradient, step - 1, False))
         finish_sends(step, STRESS_X, STRESS_Y)
-        phase(step, stress, SPEED_X, SPEED_Y, step + 1, () if last else STRESS_X, STRESS_Y)
-        if not last:
-            send_group(2 + 2 * step)
-    finish_sends(STEPS - 1, SPEED_X, SPEED_Y)
-    receive_words(STEPS - 1)
-    over(0, cx, functools.partial(gradient, STEPS - 1))
-
-
-def flush(out_in, grads_in, out, grads, sem):
-    copies = [pltpu.make_async_copy(out_in.at[index], out.at[index], sem.at[index]) for index in range(out.shape[0])]
-    copies += [pltpu.make_async_copy(grads_in.at[index], grads.at[index], sem.at[out.shape[0] + index])
-               for index in range(grads.shape[0])]
-    for copy in copies:
-        copy.start()
+        if step < final:
+            phase(step, stress, SPEED_X, SPEED_Y, step + 1, STRESS_X, STRESS_Y, 2 + 2 * step)
+    over(1, cx - 1, functools.partial(stress, final, inner))
+    receive_y(final, SPEED_Y)
+    over(1, cx - 1, functools.partial(stress, final, outer))
+    receive_words(final)
+    over(1, cx - 1, functools.partial(gradient, final, False))
+    ends(functools.partial(gradient, final, True))
+    for piece in within + outside:
+        receive_x(final, SPEED_X, piece)
+    finish_sends(final, SPEED_X, SPEED_Y)
+
+
+def finish(cur, coef, halo_y, fwd, grads_in, out, grads, s_end, g_end, sem):
+    cx, cy, cz = coef.shape[1:]
+    tile, z_before, z_after, y_before, y_after, strains, stresses = stencil(cur, coef, halo_y)
+    copies = []
+
+    def send(source, target):
+        copies.append(pltpu.make_async_copy(source, target, sem.at[len(copies)]))
+        copies[-1].start()
+
+    for field in (VX, VY, VZ):
+        send(cur.at[field, pl.ds(1, cx)], out.at[field])
+    middle = pl.ds(1, cx - 2)
+    send(cur.at[pl.ds(SXX, 6), pl.ds(2, cx - 2)], out.at[pl.ds(SXX, 6), middle])
+    send(grads_in.at[:, middle], grads.at[:, middle])
+    for end, x in enumerate((0, cx - 1)):
+        for t in range(cy // ROWS):
+            rows = pl.ds(t * ROWS, ROWS)
+            both = strains(STEPS - 1, x, t)
+            for index, value in enumerate(stresses(both, x, t)):
+                s_end[index, end, rows, :] = value
+            f = [fwd[index, x, rows, :] for index in range(6)]
+            for index, value in enumerate(products(both, f)):
+                g_end[index, end, rows, :] = grads_in[index, x, rows, :] + value
+        send(s_end.at[:, end], out.at[pl.ds(SXX, 6), x])
+        send(g_end.at[:, end], grads.at[:, x])
     for copy in copies:
         copy.wait()
 
@@ -456,14 +497,13 @@
     dma = pltpu.SemaphoreType.DMA
     held = pl.pallas_call(
         functools.partial(kernel, n_x, n_y),
-        out_shape=(pltpu.VMEM(adjoint.shape, jnp.float32), pltpu.VMEM((2, cx, cy, cz), jnp.float32)),
+        out_shape=(pltpu.VMEM((fields, cx + 2, cy, cz), jnp.float32), pltpu.VMEM((3, cx, cy, cz), jnp.float32),
+                   pltpu.VMEM((halos, cx, cz), jnp.float32), pltpu.VMEM((6, cx, cy, cz), jnp.float32),
+                   pltpu.VMEM((2, cx, cy, cz), jnp.float32)),
         in_specs=[pl.BlockSpec(memory_space=pltpu.HBM)] * 7,
-        out_specs=(pl.BlockSpec(memory_space=pltpu.VMEM),) * 2,
+        out_specs=(pl.BlockSpec(memory_space=pltpu.VMEM),) * 5,
         scratch_shapes=[
-            pltpu.VMEM((fields, cx + 2, cy, cz), jnp.float32),
-            pltpu.VMEM((3, cx, cy, cz), jnp.float32),
             pltpu.VMEM((comp, cx, cy, cz), jnp.float32),
-            pltpu.VMEM((halos, cx, cz), jnp.float32),
             pltpu.VMEM((halos, cx, cz), jnp.float32),
             pltpu.VMEM((STEPS, comp // STEPS, segw // lanes, lanes), jnp.int32),
             pltpu.VMEM((n_x, 1, comp), jnp.float32),
@@ -474,15 +514,19 @@
             dma((n_x, STEPS)), dma((n_x, STEPS)), dma((n_x,)), dma((n_x,)), dma((3 + STEPS,)),
         ] + [pltpu.VMEM((n_x, comp // STEPS, segw // lanes, lanes), jnp.int32)] * STEPS,
         compiler_params=pltpu.CompilerParams(collective_id=0, has_side_effects=True,
-                                             vmem_limit_bytes=64000000),
+                                             vmem_limit_bytes=VMEM_LIMIT),
     )(adjoint, buoyancy, lame_lambda, shear_mu, packed, scales, perm)
     return pl.pallas_call(
-        flush,
-        out_shape=tuple(jax.ShapeDtypeStruct(array.shape, jnp.float32) for array in held),
-        in_specs=[pl.BlockSpec(memory_space=pltpu.VMEM)] * 2,
+        finish,
+        out_shape=(jax.ShapeDtypeStruct(adjoint.shape, jnp.float32), jax.ShapeDtypeStruct((2, cx, cy, cz), jnp.float32)),
+        in_specs=[pl.BlockSpec(memory_space=pltpu.VMEM)] * 5,
         out_specs=(pl.BlockSpec(memory_space=pltpu.HBM),) * 2,
-        scratch_shapes=[dma((fields + 2,))],
-        compiler_params=pltpu.CompilerParams(vmem_limit_bytes=1000000),
+        scratch_shapes=[
+            pltpu.VMEM((6, 2, cy, cz), jnp.float32),
+            pltpu.VMEM((2, 2, cy, cz), jnp.float32),
+            dma((9,)),
+        ],
+        compiler_params=pltpu.CompilerParams(vmem_limit_bytes=8000000),
     )(*held)
 
 

time: 25.1 us -> 24.1 us (0.960)
  the two profiles are of different devices: /device:TPU:1 before, /device:TPU:18 now
where the time goes in v2:
time: 24.1 us; the launch traced here: 23.9 us
  Pallas kernels  23.3 us (97%)
  between operations  0.64 us (3%)
    pallas_call x1, Pallas kernels, on_device(): pl.pallas_call(functools.partial(kernel, n_x, n_y), out_shape=(pltpu.VMEM...  21.7 us
    pallas_call x1, Pallas kernels, on_device(): pl.pallas_call(finish, out_shape=(jax.ShapeDtypeStruct(adjoint.shape, jnp...  1.64 us

profile of v2, /device:TPU:18, one launch (start us, length us, event | category | flops | bytes accessed | tf_op | source)
XLA Modules:
  0.0 23.9 jit_solution(7205512311902119424)
XLA Ops:
  0.6 21.7 %shard_map.86 = (f32[9,6,32,512]{3,2,1,0:T(8,128)S(1)}, f32[3,4,32,512]{3,2,1,0:T(8,128)S(1)}, f32[12,4,512]{2,1,0:T(4,128)S(1)}, f32[6,4,32,512]{3,2,1,0:T(8,128)S(1)}, f32[2,4,32,512]{3,2,1,0:T(8,128)S(1)}) custom-call(f32[9,4,32,512]{3,2,1,0:T(8,128)} %adj.1, f32[4,32,512]{2,1,0:T(8,128)} %buoy.1, f32[4,32,512]{2,1,0:T(8,128)} %lam.1, ...), custom_call_target="tpu_custom_call" | custom-call | tf_op jit(solution)/shard_map/pallas_call | solution.py:498
  22.3 1.6 %shard_map.87 = (f32[9,4,32,512]{3,2,1,0:T(8,128)}, f32[2,4,32,512]{3,2,1,0:T(8,128)}) custom-call(f32[9,6,32,512]{3,2,1,0:T(8,128)S(1)} %get-tuple-element.7.cur, f32[3,4,32,512]{3,2,1,0:T(8,128)S(1)} %get-tuple-element.8.coef, f32[12,4,512]{2,1,0:T(4,128)S(1)} %get-tuple-element.9.halo_y, f32[6,4,32,512]{3,2,1,0:T(8,128)S(1)} %get-tuple-element.10.fwd, ...), custom_call_target="tpu_custom_call" | custom-call | tf_op jit(solution)/shard_map/pallas_call | solution.py:519

commit v3 on v2

--- a/solution.py
+++ b/solution.py
@@ -14,8 +14,8 @@
 PIECES = 2
 VMEM_LIMIT = 60500000
 TURN = 6
-BENT = (((6, 0), (4, 0), (5, 0), (2, 0), (3, 0)), ((6, 1), (7, 0), (2, 1), (1, 0)), ((4, 1), (5, 1), (3, 1), (7, 1), (1, 1)), ())
-STRAIGHT = (((4, 0), (5, 0), (6, 0), (2, 0), (3, 0)), ((4, 1), (7, 0), (2, 1), (1, 0), (0, 0)), ((5, 1), (3, 1), (6, 1), (7, 1), (1, 1)), ((0, 1),))
+BENT = (((6, 0), (4, 0), (2, 0), (3, 0)), ((5, 0), (6, 1), (2, 1), (3, 1), (1, 0)), ((4, 1), (5, 1), (7, 0), (7, 1), (1, 1)), ())
+STRAIGHT = (((4, 0), (6, 0), (2, 0)), ((5, 0), (3, 0), (7, 0), (1, 0), (0, 0)), ((4, 1), (5, 1), (2, 1), (3, 1), (6, 1), (7, 1), (1, 1)), ((0, 1),))
 
 VX, VY, VZ, SXX, SYY, SZZ, SXY, SXZ, SYZ = range(9)
 
@@ -193,9 +193,11 @@
             def _():
                 copy_x(step, message, piece).start()
 
-    def send_rows(step, messages):
+    def send_rows(step, messages, toward):
         for message in messages:
             start, fields, way = message
+            if way != toward:
+                continue
 
             @pl.when(edge(way, "gy"))
             def _():
@@ -216,9 +218,11 @@
             def _():
                 copy_y(step, message).wait_send()
 
-    def receive_y(step, messages):
+    def receive_y(step, messages, toward):
         for message in messages:
             start, fields, way = message
+            if way != toward:
+                continue
 
             @pl.when(edge(-way, "gy"))
             def _():
@@ -402,28 +406,32 @@
 
     outer = (0, tiles - 1) if tiles > 1 else (0,)
     inner = range(1, tiles - 1)
-    outside = [piece for piece in range(pieces) if set(inside(piece)) & set(outer)]
-    within = [piece for piece in range(pieces) if piece not in outside]
-
     def phase(step, body, taken, taken_y, given_step, given, given_y, group):
         over(1, cx - 1, functools.partial(body, step, inner))
-        receive_y(step, taken_y)
-        over(1, cx - 1, functools.partial(body, step, outer))
-        for piece in within + outside:
+        for piece in range(pieces):
+            rim = [t for t in inside(piece) if t in outer]
+            for t, way in ((0, 1), (tiles - 1, -1)):
+                if t in inside(piece):
+                    receive_y(step, taken_y, way)
+            if rim:
+                over(1, cx - 1, functools.partial(body, step, rim))
             receive_x(step, taken, piece)
             ends(functools.partial(body, step, inside(piece)))
             send_x(given_step, given, piece)
-        send_rows(given_step, given_y)
+            for t, way in ((0, -1), (tiles - 1, 1)):
+                if t in inside(piece):
+                    send_rows(given_step, given_y, way)
         send_group(group)
 
     for copy in edges:
         copy.wait()
-    for piece in within + outside:
+    for piece in range(pieces):
         send_x(0, STRESS_X, piece)
-    send_group(0)
     for copy in rows_in:
         copy.wait()
-    send_rows(0, STRESS_Y)
+    for way in (-1, 1):
+        send_rows(0, STRESS_Y, way)
+    send_group(0)
     perm_copy.wait()
 
     def invert(block, carry):
@@ -448,12 +456,13 @@
         if step < final:
             phase(step, stress, SPEED_X, SPEED_Y, step + 1, STRESS_X, STRESS_Y, 2 + 2 * step)
     over(1, cx - 1, functools.partial(stress, final, inner))
-    receive_y(final, SPEED_Y)
+    for way in (1, -1):
+        receive_y(final, SPEED_Y, way)
     over(1, cx - 1, functools.partial(stress, final, outer))
     receive_words(final)
     over(1, cx - 1, functools.partial(gradient, final, False))
     ends(functools.partial(gradient, final, True))
-    for piece in within + outside:
+    for piece in range(pieces):
         receive_x(final, SPEED_X, piece)
     finish_sends(final, SPEED_X, SPEED_Y)
 

time: 24.1 us -> 23.4 us (0.971)
  the two profiles are of different devices: /device:TPU:18 before, /device:TPU:1 now
where the time goes in v3:
time: 23.4 us; the launch traced here: 23.3 us
  Pallas kernels  22.6 us (97%)
  between operations  0.64 us (3%)
    pallas_call x1, Pallas kernels, on_device(): pl.pallas_call(functools.partial(kernel, n_x, n_y), out_shape=(pltpu.VMEM...  21 us
    pallas_call x1, Pallas kernels, on_device(): pl.pallas_call(finish, out_shape=(jax.ShapeDtypeStruct(adjoint.shape, jnp...  1.64 us

profile of v3, /device:TPU:1, one launch (start us, length us, event | category | flops | bytes accessed | tf_op | source)
XLA Modules:
  0.0 23.3 jit_solution(5039392801627577262)
XLA Ops:
  0.6 21.0 %shard_map.86 = (f32[9,6,32,512]{3,2,1,0:T(8,128)S(1)}, f32[3,4,32,512]{3,2,1,0:T(8,128)S(1)}, f32[12,4,512]{2,1,0:T(4,128)S(1)}, f32[6,4,32,512]{3,2,1,0:T(8,128)S(1)}, f32[2,4,32,512]{3,2,1,0:T(8,128)S(1)}) custom-call(f32[9,4,32,512]{3,2,1,0:T(8,128)} %adj.1, f32[4,32,512]{2,1,0:T(8,128)} %buoy.1, f32[4,32,512]{2,1,0:T(8,128)} %lam.1, ...), custom_call_target="tpu_custom_call" | custom-call | tf_op jit(solution)/shard_map/pallas_call | solution.py:507
  21.6 1.6 %shard_map.87 = (f32[9,4,32,512]{3,2,1,0:T(8,128)}, f32[2,4,32,512]{3,2,1,0:T(8,128)}) custom-call(f32[9,6,32,512]{3,2,1,0:T(8,128)S(1)} %get-tuple-element.7.cur, f32[3,4,32,512]{3,2,1,0:T(8,128)S(1)} %get-tuple-element.8.coef, f32[12,4,512]{2,1,0:T(4,128)S(1)} %get-tuple-element.9.halo_y, f32[6,4,32,512]{3,2,1,0:T(8,128)S(1)} %get-tuple-element.10.fwd, ...), custom_call_target="tpu_custom_call" | custom-call | tf_op jit(solution)/shard_map/pallas_call | solution.py:528

commit v4 on v3

--- a/solution.py
+++ b/solution.py
@@ -14,8 +14,9 @@
 PIECES = 2
 VMEM_LIMIT = 60500000
 TURN = 6
-BENT = (((6, 0), (4, 0), (2, 0), (3, 0)), ((5, 0), (6, 1), (2, 1), (3, 1), (1, 0)), ((4, 1), (5, 1), (7, 0), (7, 1), (1, 1)), ())
-STRAIGHT = (((4, 0), (6, 0), (2, 0)), ((5, 0), (3, 0), (7, 0), (1, 0), (0, 0)), ((4, 1), (5, 1), (2, 1), (3, 1), (6, 1), (7, 1), (1, 1)), ((0, 1),))
+RELAYED = ((6, 0), (6, 1))
+BENT = (((6, 0), (6, 1), (2, 0), (3, 0)), ((4, 0), (5, 0), (2, 1), (3, 1), (1, 0)), ((4, 1), (5, 1), (7, 0), (7, 1), (1, 1)), ())
+STRAIGHT = (((6, 0), (2, 0)), ((4, 0), (5, 0), (3, 0), (7, 0), (1, 0), (0, 0)), ((4, 1), (5, 1), (2, 1), (3, 1), (6, 1), (7, 1), (1, 1), (0, 1)), ())
 
 VX, VY, VZ, SXX, SYY, SZZ, SXY, SXZ, SYZ = range(9)
 
@@ -239,31 +240,34 @@
             def _():
                 copy_x(step, message, piece).wait_recv()
 
-    relays = n_x > TURN and n_x & (n_x - 1) == 0
+    relays = n_x > max(distance for distance, _ in RELAYED) and n_x & (n_x - 1) == 0
     bent = (me_x // (TURN & -TURN)) % 2 != (me_x // (TURN - (TURN & -TURN))) % 2
     low, high = TURN & -TURN, TURN - (TURN & -TURN)
 
-    def first_leg(step):
+    def first_leg(index):
+        distance, step = RELAYED[index]
         return pltpu.make_async_remote_copy(
-            src_ref=packed.at[partner(me_x, TURN, n_x), pl.ds(step * per_step, per_step)], dst_ref=relay.at[step],
-            send_sem=ws_sem.at[TURN, step], recv_sem=rl_sem.at[step],
+            src_ref=packed.at[partner(me_x, distance, n_x), pl.ds(step * per_step, per_step)], dst_ref=relay.at[index],
+            send_sem=ws_sem.at[distance, step], recv_sem=rl_sem.at[index],
             device_id={"gx": partner(me_x, high, n_x)}, device_id_type=MESH)
 
-    def second_leg(step):
+    def second_leg(index):
+        distance, step = RELAYED[index]
         return pltpu.make_async_remote_copy(
-            src_ref=relay.at[step], dst_ref=words[step].at[partner(me_x, high, n_x)],
-            send_sem=rf_sem.at[step], recv_sem=wr_sem.at[TURN, step],
-            device_id={"gx": partner(me_x, low, n_x)}, device_id_type=MESH)
+            src_ref=relay.at[index], dst_ref=words[step].at[partner(me_x, high, n_x)],
+            send_sem=rf_sem.at[index], recv_sem=wr_sem.at[distance, step],
+            device_id={"gx": partner(me_x, distance - high, n_x)}, device_id_type=MESH)
 
     def send_words(table, turned):
         for kind, step in table:
             if kind == 0 and relays:
                 first_leg(step).wait_recv()
                 second_leg(step).start()
+                continue
             for distance in range(1, n_x):
                 if max(distance * 8 // n_x, 1) == kind:
-                    if turned and distance == TURN:
-                        first_leg(step).start()
+                    if turned and (distance, step) in RELAYED:
+                        first_leg(RELAYED.index((distance, step))).start()
                     else:
                         word_copy(distance, step).start()
 
@@ -296,7 +300,9 @@
         if relays:
             @pl.when(jnp.logical_not(bent))
             def _():
-                second_leg(step).wait_send()
+                for index, (_, told) in enumerate(RELAYED):
+                    if told == step:
+                        second_leg(index).wait_send()
 
     tile, z_before, z_after, y_before, y_after, strains, stresses = stencil(cur, coef, halo_y)
 
@@ -514,12 +520,12 @@
         scratch_shapes=[
             pltpu.VMEM((comp, cx, cy, cz), jnp.float32),
             pltpu.VMEM((halos, cx, cz), jnp.float32),
-            pltpu.VMEM((STEPS, comp // STEPS, segw // lanes, lanes), jnp.int32),
+            pltpu.VMEM((len(RELAYED), comp // STEPS, segw // lanes, lanes), jnp.int32),
             pltpu.VMEM((n_x, 1, comp), jnp.float32),
             pltpu.SMEM((n_x, 1, comp), jnp.float32),
             pltpu.SMEM(perm.shape, jnp.int32),
             pltpu.SMEM((n_x,), jnp.int32),
-            dma((14,)), dma((STEPS,)), dma((STEPS,)), dma((halos, pieces)), dma((halos, pieces)), dma((halos,)), dma((halos,)),
+            dma((14,)), dma((len(RELAYED),)), dma((len(RELAYED),)), dma((halos, pieces)), dma((halos, pieces)), dma((halos,)), dma((halos,)),
             dma((n_x, STEPS)), dma((n_x, STEPS)), dma((n_x,)), dma((n_x,)), dma((3 + STEPS,)),
         ] + [pltpu.VMEM((n_x, comp // STEPS, segw // lanes, lanes), jnp.int32)] * STEPS,
         compiler_params=pltpu.CompilerParams(collective_id=0, has_side_effects=True,

time: 23.4 us -> 23.4 us (level)
  no operation moved by 1% of the time
where the time goes in v4:
time: 23.4 us; the launch traced here: 23.3 us
  Pallas kernels  22.6 us (97%)
  between operations  0.64 us (3%)
    pallas_call x1, Pallas kernels, on_device(): pl.pallas_call(functools.partial(kernel, n_x, n_y), out_shape=(pltpu.VMEM...  21 us
    pallas_call x1, Pallas kernels, on_device(): pl.pallas_call(finish, out_shape=(jax.ShapeDtypeStruct(adjoint.shape, jnp...  1.64 us

profile of v4, /device:TPU:1, one launch (start us, length us, event | category | flops | bytes accessed | tf_op | source)
XLA Modules:
  0.0 23.3 jit_solution(14884387683177923033)
XLA Ops:
  0.6 21.0 %shard_map.86 = (f32[9,6,32,512]{3,2,1,0:T(8,128)S(1)}, f32[3,4,32,512]{3,2,1,0:T(8,128)S(1)}, f32[12,4,512]{2,1,0:T(4,128)S(1)}, f32[6,4,32,512]{3,2,1,0:T(8,128)S(1)}, f32[2,4,32,512]{3,2,1,0:T(8,128)S(1)}) custom-call(f32[9,4,32,512]{3,2,1,0:T(8,128)} %adj.1, f32[4,32,512]{2,1,0:T(8,128)} %buoy.1, f32[4,32,512]{2,1,0:T(8,128)} %lam.1, ...), custom_call_target="tpu_custom_call" | custom-call | tf_op jit(solution)/shard_map/pallas_call | solution.py:513
  21.6 1.6 %shard_map.87 = (f32[9,4,32,512]{3,2,1,0:T(8,128)}, f32[2,4,32,512]{3,2,1,0:T(8,128)}) custom-call(f32[9,6,32,512]{3,2,1,0:T(8,128)S(1)} %get-tuple-element.7.cur, f32[3,4,32,512]{3,2,1,0:T(8,128)S(1)} %get-tuple-element.8.coef, f32[12,4,512]{2,1,0:T(4,128)S(1)} %get-tuple-element.9.halo_y, f32[6,4,32,512]{3,2,1,0:T(8,128)S(1)} %get-tuple-element.10.fwd, ...), custom_call_target="tpu_custom_call" | custom-call | tf_op jit(solution)/shard_map/pallas_call | solution.py:534
